TPU v7x, 256 devices: a whole 4x4x8 slice. The times are simulated.
256 devices in a mesh: group: 8 (over z_hi, y), shard: 32 (over x, z_lo, core).
Axes of the slice: x: 4, y: 4, z: 8 (z_hi: 2, z_lo: 4; z = z_hi * 4 + z_lo), core: 2. Of those that a mesh axis runs over, the one named last changes fastest.
Arguments:
- gradients: bfloat16 [8, 32, 256, 8192], P('group', 'shard'), may hold values from -1.59375 to 1.59375
- momentum: float32 [8, 256, 8192], P('group', None, 'shard'), may hold values from -6 to 6
- master: float32 [256, 8192], P(None, 'shard'), may hold values from -0.6 to 0.6
- indices: int32 [8, 4, 128, 32], P('group', None, 'shard'), may hold values from 0 to 4095, as said below
Outputs:
- momentum_out: float32 [8, 256, 8192], P('group', None, 'shard')
- master_out: float32 [256, 8192], P(None, 'shard')
- params_full: bfloat16 [256, 8192], replicated
Inputs may be any that keep to these rules, and one draw needn't show every extreme that they name: `indices`: the 32 positions of one group and block are distinct.
All inputs are finite; a program needn't handle non-finite values.
Results may differ from a plain program's by a relative error of at most 0.001.
Values may be sent and summed in bfloat16 or wider, within the bound.
No kernel may reach another device: no remote copies, remote signals or barrier semaphores. Data moves between devices by JAX's collectives and lax.ppermute only.
A program may use at most 128 MiB of HBM per device.

v0:
```python
import jax
import jax.numpy as jnp
from jax import lax
from jax.sharding import Mesh
from jax.sharding import PartitionSpec as P

BLOCK = 64
SHARD = ("shard_0", "shard_1", "shard_2")
momentum_decay = 0.9
step_rate = 0.5


def in_blocks(shard, dim, peers):
    before, after = (shard.shape[:dim], shard.shape[dim + 1 :])
    return jnp.moveaxis(shard.reshape(*before, peers, -1, *after), dim, 0)


def summed_rows(shard, chips, core, dim):
    sizes = (lax.axis_size(chips), lax.axis_size(core))
    parts = in_blocks(shard, dim, sizes[0] * sizes[1])
    inside = parts.shape[1:]
    parts = parts.reshape(*sizes, *inside).swapaxes(0, 1).reshape(-1, *inside)
    parts = lax.psum_scatter(parts, core, scatter_dimension=0, tiled=True)
    return lax.psum_scatter(parts, chips, scatter_dimension=0, tiled=True)[0]


def joined_along(parts, dim):
    parts = jnp.moveaxis(parts, 0, dim)
    shape = parts.shape
    return parts.reshape(*shape[:dim], shape[dim] * shape[dim + 1], *shape[dim + 2 :])


def copy_for_each(shard, axis):
    peers = lax.axis_size(axis)
    return lax.all_to_all(
        jnp.broadcast_to(shard[None], (peers, *shard.shape)), axis, 0, 0, tiled=True
    )


def gathered_copies(shard, axis, dim):
    return joined_along(copy_for_each(shard, axis), dim)


def cosine_table(side):
    freqs = jnp.arange(side, dtype=jnp.float32)[:, None]
    places = jnp.arange(side, dtype=jnp.float32)[None, :]
    table = jnp.cos(jnp.pi * (2.0 * places + 1.0) * freqs / (2.0 * side))
    weights = jnp.where(freqs == 0.0, jnp.sqrt(1.0 / side), jnp.sqrt(2.0 / side))
    return table * weights


def into_blocks(field, side):
    leading = field.shape[:-2]
    depth = len(leading)
    shaped = field.reshape(leading + (field.shape[-2] // side, side, field.shape[-1] // side, side))
    return jnp.moveaxis(shaped, depth + 2, depth + 1)


def out_blocks(blocks):
    leading = blocks.shape[:-4]
    depth = len(leading)
    moved = jnp.moveaxis(blocks, depth + 1, depth + 2)
    return moved.reshape(
        leading + (blocks.shape[-4] * blocks.shape[-2], blocks.shape[-3] * blocks.shape[-1])
    )


def forward_blocks(blocks, table):
    return jnp.einsum("kn,...nm,lm->...kl", table, blocks, table, precision=lax.Precision.HIGHEST)


def inverse_blocks(blocks, table):
    return jnp.einsum("kn,...kl,lm->...nm", table, blocks, table, precision=lax.Precision.HIGHEST)


def scatter_picked(picked, positions, target_shape):
    places = [
        lax.broadcasted_iota(jnp.int32, positions.shape, dimension)
        for dimension in range(positions.ndim - 1)
    ]
    return jnp.zeros(target_shape, picked.dtype).at[tuple(places) + (positions,)].add(picked)


def local(gradients, momentum, master, indices):
    table = cosine_table(BLOCK)
    height = master.shape[0] // BLOCK
    across = master.shape[1] // BLOCK
    local_ids = indices[0]
    local_grad = gradients[0, 0]
    summed = summed_rows(local_grad.astype(jnp.float32), ("shard_0", "shard_1"), "shard_2", 1)
    accumulated = momentum_decay * momentum[0] + summed
    coeffs = forward_blocks(into_blocks(accumulated, BLOCK), table)
    flat = coeffs.reshape(height, across, BLOCK * BLOCK)
    picked = jnp.take_along_axis(flat, local_ids, axis=2)
    own_dense = scatter_picked(picked, local_ids, flat.shape)
    momentum_out = accumulated - out_blocks(inverse_blocks(own_dense.reshape(coeffs.shape), table))
    piece_values = gathered_copies(picked[None], "group", 0)
    piece_ids = gathered_copies(local_ids[None], "group", 0)
    piece_ids = piece_ids.astype(jnp.int32)
    first = lax.broadcasted_iota(jnp.int32, piece_ids.shape, 1)
    second = lax.broadcasted_iota(jnp.int32, piece_ids.shape, 2)
    union_sum = jnp.zeros(flat.shape, jnp.float32).at[first, second, piece_ids].add(piece_values)
    change_field = out_blocks(inverse_blocks(union_sum.reshape(coeffs.shape), table))
    master_out = master - step_rate * jnp.tanh(change_field)
    params_full = lax.all_gather(master_out.astype(jnp.bfloat16), SHARD, axis=1, tiled=True)
    return (momentum_out[None], master_out, params_full)


def solution(mesh):
    torus = Mesh(
        mesh.devices.reshape(mesh.shape["group"], 4, 4, 2),
        ("group", "shard_0", "shard_1", "shard_2"),
    )
    placed = (
        P("group", SHARD, None, None),
        P("group", None, SHARD),
        P(None, SHARD),
        P("group", None, SHARD, None),
    )
    return jax.shard_map(
        local,
        mesh=torus,
        in_specs=placed,
        out_specs=(P("group", None, SHARD), P(None, SHARD), P()),
        check_vma=False,
    )
```

profile of v0, /device:TPU:1, one launch (start us, length us, event | category | flops | bytes accessed | tf_op | source)
XLA Modules:
  0.0 294.3 jit_solution(5407330677718282875)
XLA Ops:
  7.2 6.4 %copy.42 = bf16[1,1,256,8192]{2,3,1,0:T(8,128)(2,1)} copy(bf16[1,1,256,8192]{3,2,1,0:T(8,128)(2,1)} %param.4) | data formatting | bytes 8388608 | tf_op args[0]
  13.6 6.5 %convert.5 = f32[256,32,256]{0,2,1:T(8,128)} convert(bf16[256,32,256]{0,2,1:T(8,128)(2,1)} %bitcast.55) | non-fusion elementwise | flops 2097152 | bytes 12582912 | tf_op jit(solution)/shard_map/reshape | solution.py:22
  20.0 8.7 %copy.44 = f32[2,16,256,256]{3,2,1,0:T(8,128)} copy(f32[2,16,256,256]{2,3,0,1:T(8,128)} %bitcast.54) | data formatting | bytes 16777216 | tf_op jit(solution)/shard_map/reshape | solution.py:22
  28.8 26.3 %reduce-scatter.3.cloned.1.call-done = f32[16,256,256]{2,1,0:T(8,128)} async-done(((f32[32,256,256]{2,1,0:T(8,128)}), f32[16,256,256]{2,1,0:T(8,128)}) %reduce-scatter.3.cloned.1.call-update) | async-done | bytes 4194320 | tf_op jit(solution)/shard_map/reduce_scatter | solution.py:23
  55.1 0.7 reshape.197
  55.9 8.9 %all-to-all-start = ((s32[8,1,512]{2,1,0:T(1,128)}), s32[8,1,512]{2,1,0:T(1,128)S(1)}, u32[]{:S(2)}, u32[]{:S(2)}) async-start(s32[8,1,512]{2,1,0:T(1,128)} %reshape.197), calls=%async_computation.2 | async-start | bytes 32768 | tf_op jit(solution)/shard_map/all_to_all | solution.py:35
  64.9 8.9 %all-to-all-done = s32[8,1,512]{2,1,0:T(1,128)S(1)} async-done(((s32[8,1,512]{2,1,0:T(1,128)}), s32[8,1,512]{2,1,0:T(1,128)S(1)}, u32[]{:S(2)}, u32[]{:S(2)}) %all-to-all-start) | async-done | bytes 16416 | tf_op jit(solution)/shard_map/all_to_all | solution.py:35
  73.8 0.5 broadcast.241
  74.3 0.7 reduce.4
  75.4 81.4 %reduce-scatter.5.cloned.1.call-done = f32[1,256,256]{2,1,0:T(8,128)} async-done(((f32[16,256,256]{2,1,0:T(8,128)}), f32[1,256,256]{2,1,0:T(8,128)}) %reduce-scatter.5.cloned.1.call-update) | async-done | bytes 262160 | tf_op jit(solution)/shard_map/reduce_scatter | solution.py:24
  156.8 1.0 multiply_add_fusion
  158.3 1.7 fusion.2
  160.0 0.7 fusion.12
  160.9 5.3 %gather_fusion = f32[512]{0:T(512)S(1)} fusion(f32[4,4,4096]{2,1,0:T(4,128)S(1)} %reshape.156, s32[512]{0:T(512)S(1)} %reshape.173), kind=kCustom, calls=%fused_computation | custom fusion | bytes 10240 | tf_op jit(solution)/shard_map/jit(take_along_axis)/gather | solution.py:94
  166.3 0.7 reshape.199
  167.0 6.8 %all-to-all-start.1 = ((f32[8,1,512]{2,1,0:T(1,128)}), f32[8,1,512]{2,1,0:T(1,128)S(1)}, u32[]{:S(2)}, u32[]{:S(2)}) async-start(f32[8,1,512]{2,1,0:T(1,128)} %reshape.199), calls=%async_computation.3 | async-start | bytes 32768 | tf_op jit(solution)/shard_map/all_to_all | solution.py:35
  174.0 8.8 %all-to-all-done.1 = f32[8,1,512]{2,1,0:T(1,128)S(1)} async-done(((f32[8,1,512]{2,1,0:T(1,128)}), f32[8,1,512]{2,1,0:T(1,128)S(1)}, u32[]{:S(2)}, u32[]{:S(2)}) %all-to-all-start.1) | async-done | bytes 16416 | tf_op jit(solution)/shard_map/all_to_all | solution.py:35
  182.8 0.5 broadcast.242
  183.3 0.7 reduce.5
  184.2 22.2 %scatter_custom_fusion.1 = f32[65536]{0:T(1024)S(1)} fusion(s32[4096]{0:T(1024)S(1)} %reshape.185, f32[4096]{0:T(1024)S(1)} %reshape.187, f32[]{:T(128)} %constant.16.clone.1), kind=kCustom, calls=%fused_computation.14 | custom fusion | flops 4096 | bytes 262148
  206.5 0.7 fusion.7
  207.3 0.7 fusion.1
  208.0 0.3 copy.54
  208.3 0.3 mul.148
  208.7 0.8 fusion.46
  209.7 30.1 %scatter_fusion = f32[4,4,4096]{2,1,0:T(4,128)S(1)} fusion(f32[4,4,4096]{2,1,0:T(4,128)S(1)} %broadcast.160, s32[512]{0:T(512)S(1)} %reshape.179, f32[512]{0:T(512)S(1)} %reshape.181), kind=kCustom, calls=%fused_computation.1 | custom fusion | flops 512 | bytes 12288 | tf_op jit(solution)/shard_map/scatter-add | solution.py:81
  240.0 0.7 fusion.10
  240.8 0.7 convolution_bitcast_fusion
  241.8 0.3 reshape.158
  242.2 0.7 sub.7
  242.9 40.2 %all-gather.2.cloned.1.call-done = bf16[256,8192]{1,0:T(8,128)(2,1)} async-done(((bf16[256,256]{1,0:T(8,128)(2,1)}), bf16[256,8192]{1,0:T(8,128)(2,1)}) %all-gather.2.cloned.1.call-update) | async-done | bytes 4194320 | tf_op jit(solution)/shard_map/all_gather | solution.py:105
  283.2 4.6 %copy.65 = bf16[256,8192]{1,0:T(8,128)(2,1)} copy(bf16[256,8192]{1,0:T(8,128)(2,1)} %all-gather.2.cloned.1.call-done) | data formatting | bytes 8388608
  (43 shorter events, 2.7 us)
Async XLA Ops:
  7.2 47.9 %reduce-scatter.3.cloned.1.call-start = ((), (), s32[]{:S(2)}) async-start(), calls=%async_computation.4 | async-start | bytes 12582912 | tf_op jit(solution)/shard_map/reduce_scatter | solution.py:23
  28.7 26.4 %copy-start.2 = (s32[1,4,4,32]{3,2,1,0:T(4,128)S(1)}, s32[1,4,4,32]{3,2,1,0:T(4,128)}, u32[]{:S(2)}) copy-start(s32[1,4,4,32]{3,2,1,0:T(4,128)} %param.7) | copy-start | bytes 6148
  28.7 46.4 %copy-start.4 = (s32[3]{0:T(128)S(1)}, s32[3]{0:T(128)}, u32[]{:S(2)}) copy-start(s32[3]{0:T(128)} %constant.53) | copy-start | bytes 40
  28.8 46.5 %copy-start.3 = (s32[3]{0:T(128)S(1)}, s32[3]{0:T(128)}, u32[]{:S(2)}) copy-start(s32[3]{0:T(128)} %constant.56) | copy-start | bytes 40
  28.8 128.0 %copy-start = (f32[1,256,256]{2,1,0:T(8,128)S(1)}, f32[1,256,256]{2,1,0:T(8,128)}, u32[]{:S(2)}) copy-start(f32[1,256,256]{2,1,0:T(8,128)} %param.5) | copy-start | bytes 786436
  28.8 128.0 %reduce-scatter.5.cloned.1.call-start = ((), (), s32[]{:S(2)}) async-start(), calls=%async_computation.5 | async-start | bytes 4456448 | tf_op jit(solution)/shard_map/reduce_scatter | solution.py:24
  55.9 17.9 %all-to-all-start = ((s32[8,1,512]{2,1,0:T(1,128)}), s32[8,1,512]{2,1,0:T(1,128)S(1)}, u32[]{:S(2)}, u32[]{:S(2)}) async-start(s32[8,1,512]{2,1,0:T(1,128)} %reshape.197), calls=%async_computation.2 | async-start | bytes 32768 | tf_op jit(solution)/shard_map/all_to_all | solution.py:35
  166.2 42.5 %copy-start.1 = (f32[256,256]{1,0:T(8,128)S(1)}, f32[256,256]{1,0:T(8,128)}, u32[]{:S(2)}) copy-start(f32[256,256]{1,0:T(8,128)} %param.6) | copy-start | bytes 786436
  167.0 15.8 %all-to-all-start.1 = ((f32[8,1,512]{2,1,0:T(1,128)}), f32[8,1,512]{2,1,0:T(1,128)S(1)}, u32[]{:S(2)}, u32[]{:S(2)}) async-start(f32[8,1,512]{2,1,0:T(1,128)} %reshape.199), calls=%async_computation.3 | async-start | bytes 32768 | tf_op jit(solution)/shard_map/all_to_all | solution.py:35
  173.8 109.3 %all-gather.2.cloned.1.call-start = ((), (), s32[]{:S(2)}) async-start(), calls=%async_computation.6 | async-start | bytes 4325376 | tf_op jit(solution)/shard_map/all_gather | solution.py:105
Sparse Core Ops, SparseCore 0:
  28.9 26.1 reduce-scatter.2
  57.6 99.1 reduce-scatter.4
  209.6 73.5 all-gather.1
where the time goes:
time: 295 us; the launch traced here: 294 us
  waiting for transfers between devices  166 us (56%)
  other arithmetic  62.8 us (21%)
  local copies, waits for them, and re-layouts  30.7 us (10%)
  starting transfers between devices  15.8 us (5%)
  between operations  14 us (5%)
  matrix products  5.28 us (2%)
    reduce_scatter x1, waiting for transfers between devices, summed_rows(): return lax.psum_scatter(parts, chips, scatter_dimension=0, tiled=True)[0]  81.4 us
    all_gather x1, waiting for transfers between devices, local(): lax.all_gather(master_out.astype(jnp.bfloat16), SHARD, axis=1, tiled=True)  40.2 us
    scatter-add x1, other arithmetic, scatter_picked(): jnp.zeros(target_shape, picked.dtype).at[tuple(places) + (positions,)]  30.1 us
    reduce_scatter x1, waiting for transfers between devices, summed_rows(): parts = lax.psum_scatter(parts, core, scatter_dimension=0, tiled=True)  26.3 us
    unnamed x4, other arithmetic  22.4 us
    all_to_all x2, waiting for transfers between devices, copy_for_each(): lax.all_to_all(jnp.broadcast_to(shard[None], (peers, *shard.shape)), axis...  17.7 us
    all_to_all x2, starting transfers between devices, copy_for_each(): lax.all_to_all(jnp.broadcast_to(shard[None], (peers, *shard.shape)), axis...  15.7 us
    unnamed x18, local copies, waits for them, and re-layouts  12.8 us
  transfers between devices with their start and end apart: 5, of which 5 were waited for; matrix products, arithmetic and copies ran while one was open for 12% of the time, Pallas kernels for 0%

commit v1 on v0

--- a/solution.py
+++ b/solution.py
@@ -102,7 +102,12 @@
     union_sum = jnp.zeros(flat.shape, jnp.float32).at[first, second, piece_ids].add(piece_values)
     change_field = out_blocks(inverse_blocks(union_sum.reshape(coeffs.shape), table))
     master_out = master - step_rate * jnp.tanh(change_field)
-    params_full = lax.all_gather(master_out.astype(jnp.bfloat16), SHARD, axis=1, tiled=True)
+    params_full = jnp.concatenate(
+        lax.all_to_all(
+            jnp.stack([master_out.astype(jnp.bfloat16)] * lax.axis_size(SHARD)), SHARD, 0, 0
+        ),
+        axis=1,
+    )
     return (momentum_out[None], master_out, params_full)
 
 

time: 295 us -> 340 us (1.15)
  waiting for transfers between devices: 166 us -> 186 us
  starting transfers between devices: 15.8 us -> 28.7 us
  local copies, waits for them, and re-layouts: 30.7 us -> 41.3 us
    all_to_all x0 -> x1, waiting for transfers between devices: none -> 61.1 us  [local(): lax.all_to_all(jnp.stack([master_out.astype(jnp.bfloat16)] * lax.axis_siz...]
    all_gather x1 -> x0, waiting for transfers between devices: 40.2 us -> none  [local(): lax.all_gather(master_out.astype(jnp.bfloat16), SHARD, axis=1, tiled=True)]
    all_to_all x0 -> x1, starting transfers between devices: none -> 12.9 us  [local(): lax.all_to_all(jnp.stack([master_out.astype(jnp.bfloat16)] * lax.axis_siz...]
    all_to_all x0 -> x1, local copies, waits for them, and re-layouts: none -> 6.41 us  [local(): lax.all_to_all(jnp.stack([master_out.astype(jnp.bfloat16)] * lax.axis_siz...]
  transfers between devices with their start and end apart: 5 -> 5, of which waited for: 5 -> 5; matrix products, arithmetic and copies ran while one was open for 12% -> 11% of each run, Pallas kernels for 0% -> 0%
where the time goes in v1:
time: 340 us; the launch traced here: 339 us
  waiting for transfers between devices  186 us (55%)
  other arithmetic  62.6 us (18%)
  local copies, waits for them, and re-layouts  41.3 us (12%)
  starting transfers between devices  28.7 us (8%)
  between operations  14.3 us (4%)
  matrix products  5.28 us (2%)
    reduce_scatter x1, waiting for transfers between devices, summed_rows(): return lax.psum_scatter(parts, chips, scatter_dimension=0, tiled=True)[0]  81.4 us
    all_to_all x1, waiting for transfers between devices, local(): lax.all_to_all(jnp.stack([master_out.astype(jnp.bfloat16)] * lax.axis_siz...  61.1 us
    scatter-add x1, other arithmetic, scatter_picked(): jnp.zeros(target_shape, picked.dtype).at[tuple(places) + (positions,)]  30.1 us
    reduce_scatter x1, waiting for transfers between devices, summed_rows(): parts = lax.psum_scatter(parts, core, scatter_dimension=0, tiled=True)  26.3 us
    unnamed x4, other arithmetic  22.2 us
    all_to_all x2, waiting for transfers between devices, copy_for_each(): lax.all_to_all(jnp.broadcast_to(shard[None], (peers, *shard.shape)), axis...  17.7 us
    all_to_all x2, starting transfers between devices, copy_for_each(): lax.all_to_all(jnp.broadcast_to(shard[None], (peers, *shard.shape)), axis...  15.7 us
    unnamed x18, local copies, waits for them, and re-layouts  14.4 us
  transfers between devices with their start and end apart: 5, of which 5 were waited for; matrix products, arithmetic and copies ran while one was open for 11% of the time, Pallas kernels for 0%

profile of v1, /device:TPU:1, one launch (start us, length us, event | category | flops | bytes accessed | tf_op | source)
XLA Modules:
  0.0 338.7 jit_solution(10619469186513324801)
XLA Ops:
  7.2 6.4 %copy.42 = bf16[1,1,256,8192]{2,3,1,0:T(8,128)(2,1)} copy(bf16[1,1,256,8192]{3,2,1,0:T(8,128)(2,1)} %param.4) | data formatting | bytes 8388608 | tf_op args[0]
  13.6 6.5 %convert.5 = f32[256,32,256]{0,2,1:T(8,128)} convert(bf16[256,32,256]{0,2,1:T(8,128)(2,1)} %bitcast.58) | non-fusion elementwise | flops 2097152 | bytes 12582912 | tf_op jit(solution)/shard_map/reshape | solution.py:22
  20.0 8.7 %copy.44 = f32[2,16,256,256]{3,2,1,0:T(8,128)} copy(f32[2,16,256,256]{2,3,0,1:T(8,128)} %bitcast.57) | data formatting | bytes 16777216 | tf_op jit(solution)/shard_map/reshape | solution.py:22
  28.8 26.3 %reduce-scatter.3.cloned.1.call-done = f32[16,256,256]{2,1,0:T(8,128)} async-done(((f32[32,256,256]{2,1,0:T(8,128)}), f32[16,256,256]{2,1,0:T(8,128)}) %reduce-scatter.3.cloned.1.call-update) | async-done | bytes 4194320 | tf_op jit(solution)/shard_map/reduce_scatter | solution.py:23
  55.1 0.7 reshape.207
  55.9 8.9 %all-to-all-start = ((s32[8,1,512]{2,1,0:T(1,128)}), s32[8,1,512]{2,1,0:T(1,128)S(1)}, u32[]{:S(2)}, u32[]{:S(2)}) async-start(s32[8,1,512]{2,1,0:T(1,128)} %reshape.207), calls=%async_computation.2 | async-start | bytes 32768 | tf_op jit(solution)/shard_map/all_to_all | solution.py:35
  64.9 8.9 %all-to-all-done = s32[8,1,512]{2,1,0:T(1,128)S(1)} async-done(((s32[8,1,512]{2,1,0:T(1,128)}), s32[8,1,512]{2,1,0:T(1,128)S(1)}, u32[]{:S(2)}, u32[]{:S(2)}) %all-to-all-start) | async-done | bytes 16416 | tf_op jit(solution)/shard_map/all_to_all | solution.py:35
  73.8 0.5 broadcast.243
  74.3 0.7 reduce.4
  75.4 81.4 %reduce-scatter.5.cloned.1.call-done = f32[1,256,256]{2,1,0:T(8,128)} async-done(((f32[16,256,256]{2,1,0:T(8,128)}), f32[1,256,256]{2,1,0:T(8,128)}) %reduce-scatter.5.cloned.1.call-update) | async-done | bytes 262160 | tf_op jit(solution)/shard_map/reduce_scatter | solution.py:24
  156.8 1.0 multiply_add_fusion
  158.3 1.7 fusion.2
  160.0 0.7 fusion.12
  160.9 5.3 %gather_fusion = f32[512]{0:T(512)S(1)} fusion(f32[4,4,4096]{2,1,0:T(4,128)S(1)} %reshape.164, s32[512]{0:T(512)S(1)} %reshape.183), kind=kCustom, calls=%fused_computation | custom fusion | bytes 10240 | tf_op jit(solution)/shard_map/jit(take_along_axis)/gather | solution.py:94
  166.3 0.7 reshape.209
  167.0 6.8 %all-to-all-start.1 = ((f32[8,1,512]{2,1,0:T(1,128)}), f32[8,1,512]{2,1,0:T(1,128)S(1)}, u32[]{:S(2)}, u32[]{:S(2)}) async-start(f32[8,1,512]{2,1,0:T(1,128)} %reshape.209), calls=%async_computation.3 | async-start | bytes 32768 | tf_op jit(solution)/shard_map/all_to_all | solution.py:35
  174.0 8.8 %all-to-all-done.1 = f32[8,1,512]{2,1,0:T(1,128)S(1)} async-done(((f32[8,1,512]{2,1,0:T(1,128)}), f32[8,1,512]{2,1,0:T(1,128)S(1)}, u32[]{:S(2)}, u32[]{:S(2)}) %all-to-all-start.1) | async-done | bytes 16416 | tf_op jit(solution)/shard_map/all_to_all | solution.py:35
  182.8 0.5 broadcast.244
  183.3 0.7 reduce.5
  184.2 22.0 %scatter_custom_fusion.1 = f32[65536]{0:T(1024)S(1)} fusion(s32[4096]{0:T(1024)S(1)} %reshape.195, f32[4096]{0:T(1024)S(1)} %reshape.197, f32[]{:T(128)} %constant.16.clone.1), kind=kCustom, calls=%fused_computation.14 | custom fusion | flops 4096 | bytes 262148
  206.3 0.7 fusion.7
  207.1 0.7 fusion.1
  208.5 0.7 fusion.46
  209.2 2.5 stack.2
  211.7 12.9 %all-to-all-start.2 = ((bf16[32,256,256]{2,1,0:T(8,128)(2,1)}), bf16[32,256,256]{2,1,0:T(8,128)(2,1)}, u32[]{:S(2)}, u32[]{:S(2)}) async-start(bf16[32,256,256]{2,1,0:T(8,128)(2,1)} %stack.2), calls=%async_computation.4 | async-start | bytes 8388608 | tf_op jit(solution)/shard_map/all_to_all | solution.py:106
  224.8 30.1 %scatter_fusion = f32[4,4,4096]{2,1,0:T(4,128)S(1)} fusion(f32[4,4,4096]{2,1,0:T(4,128)S(1)} %broadcast.162, s32[512]{0:T(512)S(1)} %reshape.189, f32[512]{0:T(512)S(1)} %reshape.191), kind=kCustom, calls=%fused_computation.1 | custom fusion | flops 512 | bytes 12288 | tf_op jit(solution)/shard_map/scatter-add | solution.py:81
  255.2 0.8 fusion.10
  256.0 0.7 convolution_bitcast_fusion
  257.4 0.7 sub.7
  258.1 61.1 %all-to-all-done.2 = bf16[32,256,256]{2,1,0:T(8,128)(2,1)} async-done(((bf16[32,256,256]{2,1,0:T(8,128)(2,1)}), bf16[32,256,256]{2,1,0:T(8,128)(2,1)}, u32[]{:S(2)}, u32[]{:S(2)}) %all-to-all-start.2) | async-done | bytes 4194336 | tf_op jit(solution)/shard_map/all_to_all | solution.py:106
  319.1 6.4 %copy.55 = bf16[32,256,256]{1,2,0:T(8,128)(2,1)} copy(bf16[32,256,256]{2,1,0:T(8,128)(2,1)} %all-to-all-done.2) | data formatting | bytes 8388608 | tf_op jit(solution)/shard_map/all_to_all | solution.py:106
  325.6 6.3 %copy.56 = bf16[256,8192]{1,0:T(8,128)(2,1)} copy(bf16[256,8192]{0,1:T(8,128)(2,1)} %bitcast.59) | data formatting | bytes 8388608
  (44 shorter events, 3.7 us)
Async XLA Ops:
  7.2 47.9 %reduce-scatter.3.cloned.1.call-start = ((), (), s32[]{:S(2)}) async-start(), calls=%async_computation.5 | async-start | bytes 12582912 | tf_op jit(solution)/shard_map/reduce_scatter | solution.py:23
  28.7 26.4 %copy-start.2 = (s32[1,4,4,32]{3,2,1,0:T(4,128)S(1)}, s32[1,4,4,32]{3,2,1,0:T(4,128)}, u32[]{:S(2)}) copy-start(s32[1,4,4,32]{3,2,1,0:T(4,128)} %param.7) | copy-start | bytes 6148
  28.7 46.4 %copy-start.4 = (s32[3]{0:T(128)S(1)}, s32[3]{0:T(128)}, u32[]{:S(2)}) copy-start(s32[3]{0:T(128)} %constant.53) | copy-start | bytes 40
  28.8 46.5 %copy-start.3 = (s32[3]{0:T(128)S(1)}, s32[3]{0:T(128)}, u32[]{:S(2)}) copy-start(s32[3]{0:T(128)} %constant.56) | copy-start | bytes 40
  28.8 128.0 %copy-start = (f32[1,256,256]{2,1,0:T(8,128)S(1)}, f32[1,256,256]{2,1,0:T(8,128)}, u32[]{:S(2)}) copy-start(f32[1,256,256]{2,1,0:T(8,128)} %param.5) | copy-start | bytes 786436
  28.8 128.0 %reduce-scatter.5.cloned.1.call-start = ((), (), s32[]{:S(2)}) async-start(), calls=%async_computation.6 | async-start | bytes 4456448 | tf_op jit(solution)/shard_map/reduce_scatter | solution.py:24
  55.9 17.9 %all-to-all-start = ((s32[8,1,512]{2,1,0:T(1,128)}), s32[8,1,512]{2,1,0:T(1,128)S(1)}, u32[]{:S(2)}, u32[]{:S(2)}) async-start(s32[8,1,512]{2,1,0:T(1,128)} %reshape.207), calls=%async_computation.2 | async-start | bytes 32768 | tf_op jit(solution)/shard_map/all_to_all | solution.py:35
  166.2 42.3 %copy-start.1 = (f32[256,256]{1,0:T(8,128)S(1)}, f32[256,256]{1,0:T(8,128)}, u32[]{:S(2)}) copy-start(f32[256,256]{1,0:T(8,128)} %param.6) | copy-start | bytes 786436
  167.0 15.8 %all-to-all-start.1 = ((f32[8,1,512]{2,1,0:T(1,128)}), f32[8,1,512]{2,1,0:T(1,128)S(1)}, u32[]{:S(2)}, u32[]{:S(2)}) async-start(f32[8,1,512]{2,1,0:T(1,128)} %reshape.209), calls=%async_computation.3 | async-start | bytes 32768 | tf_op jit(solution)/shard_map/all_to_all | solution.py:35
  211.7 107.4 %all-to-all-start.2 = ((bf16[32,256,256]{2,1,0:T(8,128)(2,1)}), bf16[32,256,256]{2,1,0:T(8,128)(2,1)}, u32[]{:S(2)}, u32[]{:S(2)}) async-start(bf16[32,256,256]{2,1,0:T(8,128)(2,1)} %stack.2), calls=%async_computation.4 | async-start | bytes 8388608 | tf_op jit(solution)/shard_map/all_to_all | solution.py:106
Sparse Core Ops, SparseCore 0:
  28.9 26.1 reduce-scatter.2
  57.6 99.1 reduce-scatter.4
